TPU v7x, 256 devices: a whole 4x4x8 slice. The times are simulated.
256 devices in a mesh: ka: 16 (over x, z_lo, core), grid: 16 (over y, z_hi).
Axes of the slice: x: 4, y: 4, z: 8 (z_hi: 4, z_lo: 2; z = z_hi * 2 + z_lo), core: 2. Of those that a mesh axis runs over, the one named last changes fastest.
Arguments:
- orbitals: bfloat16 [16, 2, 512, 16384], P('ka', None, None, 'grid'), may hold values from -6 to 6
- potential: float32 [3, 2, 16384], P(None, None, 'grid'), may hold values from -6 to 6
- partners: int32 [3, 16], replicated, may hold values from 0 to 15, each once within a row
- occupied: int32 [16], replicated, may hold values from 128 to 512
Outputs:
- sources: bfloat16 [3, 16, 2, 512, 16384], P(None, 'ka', None, None, 'grid')
- density: float32 [3, 16384], P(None, 'grid')
Inputs may be any that keep to these rules, and one draw needn't show every extreme that they name: `partners`: each row is a permutation of the 16 k-points.
All inputs are finite; a program needn't handle non-finite values.
Results may differ from a plain program's by a relative error of at most 0.0051.
Values may be sent and summed in bfloat16 or wider, within the bound.
A program may use at most 128 MiB of HBM per device.

v0:
```python
import jax
import jax.numpy as jnp
from jax import lax
from jax.sharding import PartitionSpec as P


def filled_up(lines, peers):
    spare = -len(lines) % peers
    return jnp.pad(lines, [(0, spare)] + [(0, 0)] * (lines.ndim - 1))


def sum_in_two_steps(value, axis):
    lines = value.reshape(-1, *value.shape[1:][-1:])
    padded = filled_up(lines, lax.axis_size(axis))
    own = lax.psum_scatter(padded, axis, scatter_dimension=0, tiled=True)
    whole = lax.all_gather(own, axis, axis=0, tiled=True)
    return whole[: len(lines)].reshape(value.shape)


def from_everyone(value, axis):
    copies = jnp.broadcast_to(value, (lax.axis_size(axis), *value.shape))
    return lax.all_to_all(copies, axis, split_axis=0, concat_axis=0, tiled=True)


def over_copies(value, axis):
    return from_everyone(value, axis).sum(axis=0)


def shards(orbitals, potential, partners, occupied):
    local_count = orbitals.shape[0]
    band_count = orbitals.shape[2]
    point_count = orbitals.shape[3]
    q_count = potential.shape[0]
    k_count = partners.shape[1]
    volume_weight = 1.0 / (point_count * lax.axis_size("grid"))
    density_weight = 2.0 / (k_count * band_count)
    local_ids = lax.axis_index("ka") * local_count + jnp.arange(local_count, dtype=jnp.int32)
    k_table = jnp.arange(k_count, dtype=jnp.int32)
    local_pick = (local_ids[:, None] == k_table[None, :]).astype(jnp.int32)
    own_counts = jnp.sum(local_pick * occupied[None, :], axis=1)
    partner_ids = jnp.sum(local_pick[None, :, :] * partners[:, None, :], axis=2)
    partner_hits = (partner_ids[:, :, None] == k_table[None, None, :]).astype(jnp.int32)
    partner_counts = jnp.sum(partner_hits * occupied[None, None, :], axis=2)
    band_ids = jnp.arange(band_count, dtype=jnp.int32)
    picked = jnp.take(
        lax.all_to_all(orbitals, "ka", split_axis=3, concat_axis=0, tiled=True), partners, axis=0
    )
    fetched = lax.all_to_all(picked, "ka", split_axis=1, concat_axis=4, tiled=True)
    own_real = orbitals[:, 0].astype(jnp.float32)
    own_imag = orbitals[:, 1].astype(jnp.float32)

    def apply_field(q_index):
        real_field = potential[q_index, 0][None, None, :]
        imag_field = potential[q_index, 1][None, None, :]
        applied_real = real_field * own_real - imag_field * own_imag
        applied_imag = real_field * own_imag + imag_field * own_real
        return jnp.stack([applied_real, applied_imag], axis=1).astype(jnp.bfloat16)

    def intersection(partner_orbit, applied):
        swapped = jnp.stack([applied[:, 1], -applied[:, 0]], axis=1)
        over_real = jnp.einsum(
            "kcmg,kcng->kmn", partner_orbit, applied, preferred_element_type=jnp.float32
        )
        over_imag = jnp.einsum(
            "kcmg,kcng->kmn", partner_orbit, swapped, preferred_element_type=jnp.float32
        )
        return volume_weight * jnp.stack([over_real, over_imag], axis=1)

    applied_all = [apply_field(q_index) for q_index in range(q_count)]
    partial_all = jnp.stack(
        [intersection(fetched[q_index], applied_all[q_index]) for q_index in range(q_count)]
    )
    summed_all = sum_in_two_steps(partial_all, "grid")
    summed = [summed_all[q_index] for q_index in range(q_count)]
    own_mask = (band_ids[None, :] < own_counts[:, None]).astype(jnp.float32)
    source_list = []
    density_list = []
    for q_index in range(q_count):
        partner_orbit = fetched[q_index]
        applied = applied_all[q_index]
        partner_mask = (band_ids[None, :] < partner_counts[q_index][:, None]).astype(jnp.float32)
        masked = (summed[q_index] * partner_mask[:, None, :, None]).astype(jnp.bfloat16)
        weight_real = jnp.stack([masked[:, 0], -masked[:, 1]], axis=1)
        weight_imag = jnp.stack([masked[:, 1], masked[:, 0]], axis=1)
        mixed_real = jnp.einsum(
            "kcmg,kcmn->kng", partner_orbit, weight_real, preferred_element_type=jnp.float32
        )
        mixed_imag = jnp.einsum(
            "kcmg,kcmn->kng", partner_orbit, weight_imag, preferred_element_type=jnp.float32
        )
        projected_real = applied[:, 0].astype(jnp.float32) - mixed_real
        projected_imag = applied[:, 1].astype(jnp.float32) - mixed_imag
        source_list.append(jnp.stack([projected_real, projected_imag], axis=1).astype(jnp.bfloat16))
        density_term = jnp.sum(
            own_mask[:, :, None] * (own_real * projected_real + own_imag * projected_imag),
            axis=(0, 1),
        )
        density_list.append(density_weight * density_term)
    density = over_copies(jnp.stack(density_list), "ka")
    return (jnp.stack(source_list), density)


def solution(mesh):
    return jax.shard_map(
        shards,
        mesh=mesh,
        in_specs=(P("ka", None, None, "grid"), P(None, None, "grid"), P(), P()),
        out_specs=(P(None, "ka", None, None, "grid"), P(None, "grid")),
        check_vma=False,
    )
```

profile of v0, /device:TPU:1, one launch (start us, length us, event | category | flops | bytes accessed | tf_op | source)
XLA Modules:
  0.0 432.0 jit_solution(4472959175566791039)
XLA Ops:
  7.2 6.2 %copy.66 = bf16[1,2,512,1024]{2,1,0,3:T(2,128)(2,1)} copy(bf16[1,2,512,1024]{3,2,1,0:T(8,128)(2,1)} %param.4) | data formatting | bytes 4194304 | tf_op args[0]
  13.3 7.3 %all-to-all-start = ((bf16[1,2,512,1024]{2,1,0,3:T(2,128)(2,1)}), bf16[1,2,512,1024]{2,1,0,3:T(2,128)(2,1)S(1)}, u32[]{:S(2)}, u32[]{:S(2)}) async-start(bf16[1,2,512,1024]{2,1,0,3:T(2,128)(2,1)} %copy.66), calls=%async_computation | async-start | bytes 4194304 | tf_op jit(solution)/shard_map/all_to_all | solution.py:46
  20.8 26.7 %all-to-all-done = bf16[1,2,512,1024]{2,1,0,3:T(2,128)(2,1)S(1)} async-done(((bf16[1,2,512,1024]{2,1,0,3:T(2,128)(2,1)}), bf16[1,2,512,1024]{2,1,0,3:T(2,128)(2,1)S(1)}, u32[]{:S(2)}, u32[]{:S(2)}) %all-to-all-start) | async-done | bytes 2097184 | tf_op jit(solution)/shard_map/all_to_all | solution.py:46
  47.6 1.3 copy-done.3
  48.9 2.0 copy.105
  50.9 5.0 %gather_fusion = bf16[48,2,512,64]{2,3,1,0:T(8,128)(2,1)} fusion(bf16[16,2,512,64]{2,3,1,0:T(8,128)(2,1)S(1)} %bitcast.194, s32[1024]{0:T(1024)S(1)} %pad_clamp_fusion), kind=kCustom, calls=%fused_computation | custom fusion | bytes 12583104 | tf_op jit(solution)/shard_map/jit(_take)/gather | solution.py:45
  55.9 3.4 broadcast_select_fusion
  59.4 3.4 copy.69
  62.8 5.5 %all-to-all-start.1 = ((bf16[3,16,2,512,64]{3,4,2,0,1:T(8,128)(2,1)}), bf16[3,16,2,512,64]{3,4,2,0,1:T(8,128)(2,1)}, u32[]{:S(2)}, u32[]{:S(2)}) async-start(bf16[3,16,2,512,64]{3,4,2,0,1:T(8,128)(2,1)} %copy.69), calls=%async_computation.1 | async-start | bytes 12582912 | tf_op jit(solution)/shard_map/all_to_all | solution.py:48
  68.6 2.4 fusion.18
  71.0 3.5 fusion.90
  74.5 65.9 %all-to-all-done.1 = bf16[3,16,2,512,64]{3,4,2,0,1:T(8,128)(2,1)} async-done(((bf16[3,16,2,512,64]{3,4,2,0,1:T(8,128)(2,1)}), bf16[3,16,2,512,64]{3,4,2,0,1:T(8,128)(2,1)}, u32[]{:S(2)}, u32[]{:S(2)}) %all-to-all-start.1) | async-done | bytes 6291488 | tf_op jit(solution)/shard_map/all_to_all | solution.py:48
  140.4 3.5 copy.104
  144.0 0.7 fusion.97
  145.5 1.3 fusion.52
  146.8 0.7 copy-done.16
  147.5 1.3 fusion.53
  149.0 1.3 fusion.56
  150.4 1.3 fusion.57
  151.9 1.3 fusion.48
  153.2 1.3 fusion.49
  154.7 0.7 maximum_multiply_fusion
  155.5 3.4 pad_maximum_fusion
  158.9 110.0 %reduce-scatter.2.cloned.1.call-done = f32[192,512]{1,0:T(8,128)} async-done(((f32[3072,512]{1,0:T(8,128)}), f32[192,512]{1,0:T(8,128)}) %reduce-scatter.2.cloned.1.call-update) | async-done | bytes 393232 | tf_op jit(solution)/shard_map/reduce_scatter | solution.py:15
  269.2 0.7 fusion.99
  270.5 0.7 fusion.73
  273.2 88.4 %all-gather.2.cloned.1.call-done = f32[3072,512]{1,0:T(8,128)} async-done(((f32[192,512]{1,0:T(8,128)}), f32[3072,512]{1,0:T(8,128)}) %all-gather.2.cloned.1.call-update) | async-done | bytes 6291472 | tf_op jit(solution)/shard_map/all_gather | solution.py:16
  361.6 5.7 %fusion.96 = (f32[1024,512]{1,0:T(8,128)}, f32[1024,512]{1,0:T(8,128)}, f32[1024,512]{1,0:T(8,128)}) fusion(f32[3072,512]{1,0:T(8,128)} %all-gather.2.cloned.1.call-done), kind=kLoop, calls=%fused_computation.152 | loop fusion | bytes 12582912 | tf_op jit(solution)/shard_map/slice | solution.py:74
  367.3 2.9 copy.83
  370.2 2.0 multiply_convert_fusion
  372.3 1.5 copy-done.11
  373.8 2.6 convert_subtract_fusion.1
  376.4 2.6 convert_subtract_fusion
  379.0 2.9 copy.80
  381.9 2.0 multiply_convert_fusion.1
  384.0 1.5 copy-done.9
  385.4 2.6 convert_subtract_fusion.3
  388.1 2.7 convert_subtract_fusion.2
  390.7 2.9 copy.77
  393.7 2.0 multiply_convert_fusion.2
  395.8 1.5 copy-done.2
  397.2 1.3 convert_subtract_fusion.4
  400.2 4.4 %fusion.8 = (f32[1024]{0:T(1024)S(1)}, f32[1024]{0:T(1024)S(1)}, f32[1024]{0:T(1024)S(1)}, bf16[1,1,1,512,1024]{4,3,2,1,0:T(8,128)(2,1)}, bf16[1,1,1,512,1024]{4...) fusion(f32[512,1024]{1,0:T(8,128)S(1)} %convert_subtract_fusion, ...), kind=kOutput, calls=%fused_computation.27 | convolution fusion | flops 1087370240 | bytes 23083008 | tf_op jit(solution)/shard_map/kcmg,kcmn->kng/dot_general | solution.py:85
  404.6 0.7 broadcast_in_dim.17
  405.4 12.0 %all-to-all-start.2 = ((f32[16,3,1024]{2,1,0:T(4,128)}), f32[16,3,1024]{2,1,0:T(4,128)S(1)}, u32[]{:S(2)}, u32[]{:S(2)}) async-start(f32[16,3,1024]{2,1,0:T(4,128)} %broadcast_in_dim.17), calls=%async_computation.3 | async-start | bytes 524288 | tf_op jit(solution)/shard_map/all_to_all | solution.py:22
  417.3 6.4 %maximum_maximum_fusion = bf16[3,1,2,512,1024]{4,3,2,1,0:T(8,128)(2,1)} fusion(bf16[1,1,1,512,1024]{4,3,2,1,0:T(8,128)(2,1)} %get-tuple-element.18, bf16[1,1,1,512,1024]{4,3,2,1,0:T(8,128)(2,1)} %get-tuple-element.17, bf16[1,1,1,512,1024]{4,3,2,1,0:T(8,128)(2,1)} %get-tuple-element.20, bf16[1,1,1,512,1024]{4,3,2,1,0:T(8,128)(2,1)} %get-tuple-element.19, ...), kind=kLoop, calls=%fused_computation.2 | loop fusion | flops 15728640 | bytes 12582912 | tf_op jit(solution)/shard_map/stack | solution.py:100
  423.7 0.8 all-to-all-done.2
  424.5 0.7 reduce_sum.69
  (74 shorter events, 6.9 us)
Async XLA Ops:
  13.3 7.3 %copy-start.26 = (s32[3,16]{1,0:T(4,128)S(1)}, s32[3,16]{1,0:T(4,128)}, u32[]{:S(2)}) copy-start(s32[3,16]{1,0:T(4,128)} %param.6) | copy-start | bytes 580
  13.3 34.2 %all-to-all-start = ((bf16[1,2,512,1024]{2,1,0,3:T(2,128)(2,1)}), bf16[1,2,512,1024]{2,1,0,3:T(2,128)(2,1)S(1)}, u32[]{:S(2)}, u32[]{:S(2)}) async-start(bf16[1,2,512,1024]{2,1,0,3:T(2,128)(2,1)} %copy.66), calls=%async_computation | async-start | bytes 4194304 | tf_op jit(solution)/shard_map/all_to_all | solution.py:46
  47.6 1.3 copy-start.3
  62.8 5.7 %copy-start.25 = (f32[3,2,1024]{2,1,0:T(2,128)S(1)}, f32[3,2,1024]{2,1,0:T(2,128)}, u32[]{:S(2)}) copy-start(f32[3,2,1024]{2,1,0:T(2,128)} %param.5) | copy-start | bytes 73732
  62.8 5.8 %copy-start = (bf16[1,2,512,1024]{3,2,1,0:T(8,128)(2,1)S(1)}, bf16[1,2,512,1024]{3,2,1,0:T(8,128)(2,1)}, u32[]{:S(2)}) copy-start(bf16[1,2,512,1024]{3,2,1,0:T(8,128)(2,1)} %param.4) | copy-start | bytes 6291460
  62.8 77.6 %all-to-all-start.1 = ((bf16[3,16,2,512,64]{3,4,2,0,1:T(8,128)(2,1)}), bf16[3,16,2,512,64]{3,4,2,0,1:T(8,128)(2,1)}, u32[]{:S(2)}, u32[]{:S(2)}) async-start(bf16[3,16,2,512,64]{3,4,2,0,1:T(8,128)(2,1)} %copy.69), calls=%async_computation.1 | async-start | bytes 12582912 | tf_op jit(solution)/shard_map/all_to_all | solution.py:48
  68.3 200.6 %reduce-scatter.2.cloned.1.call-start = ((), (), s32[]{:S(2)}) async-start(), calls=%async_computation.4 | async-start | bytes 6684672 | tf_op jit(solution)/shard_map/reduce_scatter | solution.py:15
  143.9 1.2 copy-start.14
  143.9 1.5 copy-start.24
  144.7 2.1 copy-start.8
  144.7 5.6 %copy-start.1 = (bf16[1,1,2,512,16,64]{3,5,4,2,1,0:T(8,128)(2,1)}, bf16[1,1,2,512,16,64]{3,5,4,2,1,0:T(8,128)(2,1)S(1)}, u32[]{:S(2)}) copy-start(bf16[1,1,2,512,16,64]{3,5,4,2,1,0:T(8,128)(2,1)S(1)} %get-tuple-element.14) | copy-start | bytes 6291460
  144.7 8.5 %copy-start.10 = (bf16[1,1,2,512,16,64]{3,5,4,2,1,0:T(8,128)(2,1)}, bf16[1,1,2,512,16,64]{3,5,4,2,1,0:T(8,128)(2,1)S(1)}, u32[]{:S(2)}) copy-start(bf16[1,1,2,512,16,64]{3,5,4,2,1,0:T(8,128)(2,1)S(1)} %get-tuple-element.15) | copy-start | bytes 6291460
  145.5 2.0 copy-start.16
  147.5 1.3 copy-start.12
  147.5 1.5 copy-start.23
  150.3 1.3 copy-start.18
  150.3 1.5 copy-start.22
  151.9 1.3 copy-start.20
  158.9 110.1 %copy-start.27 = (s32[16]{0:T(128)S(1)}, s32[16]{0:T(128)}, u32[]{:S(2)}) copy-start(s32[16]{0:T(128)} %param.7) | copy-start | bytes 196
  158.9 202.7 %all-gather.2.cloned.1.call-start = ((), (), s32[]{:S(2)}) async-start(), calls=%async_computation.5 | async-start | bytes 6684672 | tf_op jit(solution)/shard_map/all_gather | solution.py:16
  370.2 2.1 copy-start.21
  372.2 1.6 copy-start.11
  373.8 2.6 copy-start.19
  381.9 2.1 copy-start.17
  383.8 1.6 copy-start.9
  385.4 2.6 copy-start.15
  393.7 2.1 copy-start.13
  395.6 1.6 copy-start.2
  395.6 2.9 copy-start.7
  397.2 1.7 copy-start.4
  397.2 2.4 copy-start.5
  397.2 3.0 copy-start.6
  405.4 19.2 %all-to-all-start.2 = ((f32[16,3,1024]{2,1,0:T(4,128)}), f32[16,3,1024]{2,1,0:T(4,128)S(1)}, u32[]{:S(2)}, u32[]{:S(2)}) async-start(f32[16,3,1024]{2,1,0:T(4,128)} %broadcast_in_dim.17), calls=%async_computation.3 | async-start | bytes 524288 | tf_op jit(solution)/shard_map/all_to_all | solution.py:22
Sparse Core Ops, SparseCore 0:
  159.0 109.8 reduce-scatter.1
  271.4 90.1 all-gather.1
where the time goes:
time: 433 us; the launch traced here: 432 us
  waiting for transfers between devices  292 us (67%)
  local copies, waits for them, and re-layouts  46.2 us (11%)
  other arithmetic  30.6 us (7%)
  starting transfers between devices  25 us (6%)
  matrix products  23.9 us (6%)
  between operations  14.5 us (3%)
    reduce_scatter x1, waiting for transfers between devices, sum_in_two_steps(): own = lax.psum_scatter(padded, axis, scatter_dimension=0, tiled=True)  110 us
    all_gather x1, waiting for transfers between devices, sum_in_two_steps(): whole = lax.all_gather(own, axis, axis=0, tiled=True)  88.4 us
    all_to_all x1, waiting for transfers between devices, shards(): lax.all_to_all(picked, 'ka', split_axis=1, concat_axis=4, tiled=True)  65.9 us
    all_to_all x1, waiting for transfers between devices, shards(): lax.all_to_all(orbitals, 'ka', split_axis=3, concat_axis=0, tiled=True)  26.7 us
    unnamed x57, local copies, waits for them, and re-layouts  15.5 us
    all_to_all x1, starting transfers between devices, from_everyone(): return lax.all_to_all(copies, axis, split_axis=0, concat_axis=0, tiled=True)  12 us
    dot_general x3, matrix products, shards(): jnp.einsum('kcmg,kcmn->kng', partner_orbit, weight_real, preferred_elemen...  9.65 us
    squeeze x3, local copies, waits for them, and re-layouts, shards(): summed = [summed_all[q_index] for q_index in range(q_count)]  8.73 us
  transfers between devices with their start and end apart: 5, of which 5 were waited for; matrix products, arithmetic and copies ran while one was open for 4% of the time, Pallas kernels for 0%

commit v1 on v0

v1 whole, which is shorter than its diff:
```python
import functools

import jax
import jax.numpy as jnp
from jax import lax
from jax.experimental import pallas as pl
from jax.experimental.pallas import tpu as pltpu
from jax.sharding import PartitionSpec as P

MESH = pl.DeviceIdType.MESH
BLOCKS = 2


def remote(src, dst, send_sem, recv_sem, target):
    return pltpu.make_async_remote_copy(
        src_ref=src,
        dst_ref=dst,
        send_sem=send_sem,
        recv_sem=recv_sem,
        device_id=target,
        device_id_type=MESH,
    )


def dot(a, b, dims):
    return lax.dot_general(a, b, (dims, ((), ())), preferred_element_type=jnp.float32)


def kernel(
    sizes,
    partners,
    occupied,
    orbitals,
    potential,
    sources,
    density,
    held,
    picked,
    partner,
    applied,
    whole,
    ysend,
    yrecv,
    quarter,
    zsend,
    zrecv,
    masked,
    mixer,
    result,
    shares,
    sems,
):
    K, NY, NZ, Q, H = sizes
    _, _, B, G = orbitals.shape
    NX, J = K // 4, K // 2
    M = B // H
    R = M // J
    YN = B // NY
    ZN = YN // NZ
    volume_weight = 1.0 / (G * NY * NZ)
    density_weight = 2.0 / (K * B)
    units = [(q, h) for h in range(H) for q in range(Q)]

    ka = lax.axis_index("ka")
    gr = lax.axis_index("grid")
    x, low, core = lax.div(ka, 4), lax.rem(lax.div(ka, 2), 2), lax.rem(ka, 2)
    y, z = lax.div(gr, NZ), lax.rem(gr, NZ)

    order = [(0, 1)]
    for dx in [1, NX - 1, 2]:
        for dc in (0, 1):
            if 0 < dx < NX and (dx, dc) not in order:
                order.append((dx, dc))

    def plane(dx, dc):
        px, pc = lax.rem(x + dx + NX, NX), lax.rem(core + dc + 2, 2)
        return px * 4 + low * 2 + pc, px * 2 + pc

    mine = x * 2 + core
    beside = (x * 4 + (1 - low) * 2 + core, gr)

    def y_peer(d):
        return lax.rem(y + d, NY)

    def z_peer(d):
        return lax.rem(z + d, NZ)

    barrier = pltpu.get_barrier_semaphore()
    greeted = [(lax.rem(ka + d, K), gr) for d in range(1, K)]
    greeted += [(ka, y_peer(d) * NZ + z) for d in range(1, NY)]
    greeted += [(ka, y * NZ + z_peer(d)) for d in range(1, NZ)]
    for target in greeted:
        pl.semaphore_signal(barrier, inc=1, device_id=target, device_id_type=MESH)
    pl.semaphore_wait(barrier, len(greeted))

    def rows(h, piece):
        return pl.ds(pl.multiple_of(h * M + piece * R, R), R)

    for h in range(H):
        for i, (dx, dc) in enumerate(order):
            pk, pj = plane(dx, dc)
            remote(
                orbitals.at[0, :, rows(h, pj), :],
                held[h].at[ka],
                sems["spread_s"].at[h],
                sems["spread_r"].at[h, i],
                (pk, gr),
            ).start()

    def apply_field(q):
        real, imag = potential[q, 0:1, :], potential[q, 1:2, :]

        def strip(t, _):
            at = pl.ds(pl.multiple_of(t * 64, 64), 64)
            under = pl.ds(pl.multiple_of(B + t * 64, 64), 64)
            own_real = orbitals[0, 0, at, :].astype(jnp.float32)
            own_imag = orbitals[0, 1, at, :].astype(jnp.float32)
            applied[q, at, :] = (real * own_real - imag * own_imag).astype(jnp.bfloat16)
            applied[q, under, :] = (real * own_imag + imag * own_real).astype(jnp.bfloat16)
            return 0

        lax.fori_loop(0, B // 64, strip, 0)

    def relay(h, slot, source):
        remote(
            source, held[h].at[slot], sems["relay_s"].at[h], sems["relay_r"].at[h], beside
        ).start()

    for h in range(H):
        relay(h, ka, orbitals.at[0, :, rows(h, mine), :])
        held[h][ka] = orbitals[0, :, rows(h, mine), :]
        for q in range(Q):
            if q % H == h:
                apply_field(q)
        for i, (dx, dc) in enumerate(order):
            slot, _ = plane(-dx, -dc)
            remote(
                held[h].at[slot],
                held[h].at[slot],
                sems["spread_s"].at[h],
                sems["spread_r"].at[h, i],
                beside,
            ).wait_recv()
            relay(h, slot, held[h].at[slot])

    def wait_relay(h):
        block = held[h].at[pl.ds(0, J)]
        remote(block, block, sems["relay_s"].at[h], sems["relay_r"].at[h], beside).wait_recv()

    def hand_out(h):
        for q in range(Q):
            u = h * Q + q
            for i, (dx, dc) in enumerate(order):
                pk, _ = plane(dx, dc)
                picked[u, i] = held[h][partners[q, pk]]
            partner[q, :, rows(h, mine), :] = held[h][partners[q, ka]]
            for i, (dx, dc) in enumerate(order):
                pk, _ = plane(dx, dc)
                remote(
                    picked.at[u, i],
                    partner.at[q, :, rows(h, mine), :],
                    sems["hand_s"].at[u],
                    sems["hand_r"].at[u],
                    (pk, gr),
                ).start()

    def intersect(u):
        q, h = units[u]
        block = partner.at[q, :, pl.ds(h * M, (J - 1) * R), :]
        remote(block, block, sems["hand_s"].at[u], sems["hand_r"].at[u], beside).wait_recv()
        last = ((1,), (1,))
        field = applied[q]
        with_real = dot(field, partner[q, 0, h * M : (h + 1) * M, :], last)
        with_imag = dot(field, partner[q, 1, h * M : (h + 1) * M, :], last)
        real = volume_weight * (with_real[:B] + with_imag[B:])
        imag = volume_weight * (with_real[B:] - with_imag[:B])
        for part, value in enumerate((real, imag)):
            value = value.reshape(NY, YN, M)
            whole[:, part] = value
            ysend[u, :, part] = value.astype(jnp.bfloat16)
        for d in range(1, NY):
            remote(
                ysend.at[u, y_peer(d)],
                yrecv.at[u, d - 1],
                sems["y_s"].at[u],
                sems["y_r"].at[u],
                (ka, y_peer(d) * NZ + z),
            ).start()

    def sum_y(u):
        if NY > 1:
            block = yrecv.at[u]
            remote(block, block, sems["y_s"].at[u], sems["y_r"].at[u], beside).wait_recv()
        for t in range(NZ):
            value = whole[y, :, t * ZN : (t + 1) * ZN, :]
            for d in range(NY - 1):
                value = value + yrecv[u, d, :, t * ZN : (t + 1) * ZN, :].astype(jnp.float32)
            quarter[t] = value
            zsend[u, t] = value.astype(jnp.bfloat16)
        for d in range(1, NZ):
            remote(
                zsend.at[u, z_peer(d)],
                zrecv.at[u, d - 1],
                sems["z_s"].at[u],
                sems["z_r"].at[u],
                (ka, y * NZ + z_peer(d)),
            ).start()

    def sum_z(u):
        q, h = units[u]
        if NZ > 1:
            block = zrecv.at[u]
            remote(block, block, sems["z_s"].at[u], sems["z_r"].at[u], beside).wait_recv()
        value = quarter[z]
        for d in range(NZ - 1):
            value = value + zrecv[u, d].astype(jnp.float32)
        bands = h * M + lax.broadcasted_iota(jnp.int32, value.shape, 2)
        count = occupied[partners[q, ka]]
        masked[u, y, z] = jnp.where(bands < count, value, 0.0).astype(jnp.bfloat16)
        for d in range(1, NZ):
            remote(
                masked.at[u, y, z],
                masked.at[u, y, z],
                sems["zz_s"].at[u],
                sems["zz_r"].at[u],
                (ka, y * NZ + z_peer(d)),
            ).start()

    def gather_z(u):
        if NZ > 1:
            block = masked.at[u, 0, pl.ds(0, NZ - 1)]
            remote(block, block, sems["zz_s"].at[u], sems["zz_r"].at[u], beside).wait_recv()
        for d in range(1, NY):
            remote(
                masked.at[u, y],
                masked.at[u, y],
                sems["yy_s"].at[u],
                sems["yy_r"].at[u],
                (ka, y_peer(d) * NZ + z),
            ).start()

    def gather_y(u):
        q, h = units[u]
        if NY > 1:
            block = masked.at[u, pl.ds(0, NY - 1)]
            remote(block, block, sems["yy_s"].at[u], sems["yy_r"].at[u], beside).wait_recv()
        real = masked[u, :, :, 0].reshape(B, M)
        imag = masked[u, :, :, 1].reshape(B, M)
        mixer[q, 0:B, h * M : (h + 1) * M] = real
        mixer[q, 0:B, B + h * M : B + (h + 1) * M] = -imag
        mixer[q, B : 2 * B, h * M : (h + 1) * M] = imag
        mixer[q, B : 2 * B, B + h * M : B + (h + 1) * M] = real

    def out_copy(q):
        return pltpu.make_async_copy(result.at[q], sources.at[q, 0], sems["out"].at[q])

    def project(q):
        own_count = occupied[ka]
        width = 256

        def strip(t, _):
            at = pl.ds(pl.multiple_of(t * width, width), width)
            mixed = dot(mixer[q], partner[q, :, :, at].reshape(2 * B, width), ((1,), (0,)))
            real = applied[q, 0:B, at].astype(jnp.float32) - mixed[:B]
            imag = applied[q, B : 2 * B, at].astype(jnp.float32) - mixed[B:]
            result[q, 0, :, at] = real.astype(jnp.bfloat16)
            result[q, 1, :, at] = imag.astype(jnp.bfloat16)
            term = orbitals[0, 0, :, at].astype(jnp.float32) * real
            term = term + orbitals[0, 1, :, at].astype(jnp.float32) * imag
            bands = lax.broadcasted_iota(jnp.int32, term.shape, 0)
            term = jnp.where(bands < own_count, term, 0.0)
            shares[q, ka, :, at] = density_weight * jnp.sum(term, axis=0, keepdims=True)
            return 0

        lax.fori_loop(0, G // width, strip, 0)
        out_copy(q).start()
        for d in range(1, K):
            remote(
                shares.at[q, ka],
                shares.at[q, ka],
                sems["share_s"].at[q],
                sems["share_r"].at[q],
                (lax.rem(ka + d, K), gr),
            ).start()

    wait_relay(0)
    hand_out(0)
    count = len(units)
    for u in range(count + 2):
        if u < count:
            intersect(u)
        if 1 <= u <= count:
            sum_z(u - 1)
        if 2 <= u:
            gather_y(u - 2)
            q, h = units[u - 2]
            if h == H - 1:
                project(q)
        if 1 <= u <= count:
            gather_z(u - 1)
        if u < count:
            sum_y(u)
        if u % Q == 1 and u // Q + 1 < H:
            wait_relay(u // Q + 1)
            hand_out(u // Q + 1)

    for q in range(Q):
        block = shares.at[q, pl.ds(0, K - 1)]
        remote(block, block, sems["share_s"].at[q], sems["share_r"].at[q], beside).wait_recv()
        density[q : q + 1, :] = jnp.sum(shares[q], axis=0)

    def sent(block, sem):
        remote(block, block, sem, sem, beside).wait_send()

    for q in range(Q):
        out_copy(q).wait()
        sent(shares.at[q, pl.ds(0, K - 1)], sems["share_s"].at[q])
    for h in range(H):
        sent(held[h].at[pl.ds(0, J - 1)], sems["spread_s"].at[h])
        sent(held[h].at[pl.ds(0, J)], sems["relay_s"].at[h])
    for u in range(count):
        sent(picked.at[u], sems["hand_s"].at[u])
        if NY > 1:
            sent(yrecv.at[u], sems["y_s"].at[u])
            sent(masked.at[u, pl.ds(0, NY - 1)], sems["yy_s"].at[u])
        if NZ > 1:
            sent(zrecv.at[u], sems["z_s"].at[u])
            sent(masked.at[u, 0, pl.ds(0, NZ - 1)], sems["zz_s"].at[u])


def shards(sizes, orbitals, potential, partners, occupied):
    K, NY, NZ, Q, H = sizes
    _, _, B, G = orbitals.shape
    J, M = K // 2, B // H
    R, YN = M // J, B // NY
    ZN, U = YN // NZ, Q * H
    half, full = jnp.bfloat16, jnp.float32
    DMA = pltpu.SemaphoreType.DMA
    sems = {name: DMA((U,)) for part in ("hand", "y", "z", "zz", "yy") for name in (part + "_s", part + "_r")}
    sems |= {"spread_s": DMA((H,)), "spread_r": DMA((H, J)), "relay_s": DMA((H,)), "relay_r": DMA((H,))}
    sems |= {"share_s": DMA((Q,)), "share_r": DMA((Q,)), "out": DMA((Q,))}
    scratch = dict(
        held=[pltpu.VMEM((K, 2, R, G), half) for _ in range(H)],
        picked=pltpu.VMEM((U, J - 1, 2, R, G), half),
        partner=pltpu.VMEM((Q, 2, B, G), half),
        applied=pltpu.VMEM((Q, 2 * B, G), half),
        whole=pltpu.VMEM((NY, 2, YN, M), full),
        ysend=pltpu.VMEM((U, NY, 2, YN, M), half),
        yrecv=pltpu.VMEM((U, max(NY - 1, 1), 2, YN, M), half),
        quarter=pltpu.VMEM((NZ, 2, ZN, M), full),
        zsend=pltpu.VMEM((U, NZ, 2, ZN, M), half),
        zrecv=pltpu.VMEM((U, max(NZ - 1, 1), 2, ZN, M), half),
        masked=pltpu.VMEM((U, NY, NZ, 2, ZN, M), half),
        mixer=pltpu.VMEM((Q, 2 * B, 2 * B), half),
        result=pltpu.VMEM((Q, 2, B, G), half),
        shares=pltpu.VMEM((Q, K, 1, G), full),
        sems=sems,
    )
    vmem = pl.BlockSpec(memory_space=pltpu.VMEM)
    smem = pl.BlockSpec(memory_space=pltpu.SMEM)
    return pl.pallas_call(
        functools.partial(kernel, sizes),
        out_shape=(
            jax.ShapeDtypeStruct((Q, 1, 2, B, G), half),
            jax.ShapeDtypeStruct((Q, G), full),
        ),
        in_specs=[smem, smem, vmem, vmem],
        out_specs=(pl.BlockSpec(memory_space=pl.ANY), vmem),
        scratch_shapes=scratch,
        compiler_params=pltpu.CompilerParams(
            collective_id=0, has_side_effects=True, vmem_limit_bytes=64 * 1024 * 1024 - 65536
        ),
    )(partners, occupied, orbitals, potential)


def solution(mesh, ways=None):
    K, points = mesh.shape["ka"], mesh.shape["grid"]
    NY, NZ = ways or (4, points // 4)

    def local(orbitals, potential, partners, occupied):
        sizes = (K, NY, NZ, potential.shape[0], BLOCKS)
        return shards(sizes, orbitals, potential, partners, occupied)

    return jax.shard_map(
        local,
        mesh=mesh,
        in_specs=(P("ka", None, None, "grid"), P(None, None, "grid"), P(), P()),
        out_specs=(P(None, "ka", None, None, "grid"), P(None, "grid")),
        check_vma=False,
    )
```

time: 433 us -> 161 us (0.37)
  waiting for transfers between devices: 292 us -> 0 us
  Pallas kernels: 0 us -> 153 us
  local copies, waits for them, and re-layouts: 46.2 us -> 7.49 us
  other arithmetic: 30.6 us -> 0 us
  starting transfers between devices: 25 us -> 0 us
  matrix products: 23.9 us -> 0 us
  between operations: 14.5 us -> 0.65 us
    pallas_call x0 -> x1, Pallas kernels: none -> 153 us  [shards(): pl.pallas_call(functools.partial(kernel, sizes), out_shape=(jax.ShapeDtyp...]
    reduce_scatter x1 -> x0, waiting for transfers between devices: 110 us -> none  [sum_in_two_steps(): own = lax.psum_scatter(padded, axis, scatter_dimension=0, tiled=True)]
    all_to_all x3 -> x0, waiting for transfers between devices: 93.4 us -> none  [the longest x1 65.9 us: shards(): lax.all_to_all(picked, 'ka', split_axis=1, concat_axis=4, tiled=True)]
    all_gather x1 -> x0, waiting for transfers between devices: 88.4 us -> none  [sum_in_two_steps(): whole = lax.all_gather(own, axis, axis=0, tiled=True)]
    all_to_all x3 -> x0, starting transfers between devices: 24.7 us -> none  [the longest x1 12 us: from_everyone(): return lax.all_to_all(copies, axis, split_axis=0, concat_axis=0, tiled=True)]
    dot_general x12 -> x0, matrix products: 23.9 us -> none  [the longest x3 9.65 us: shards(): jnp.einsum('kcmg,kcmn->kng', partner_orbit, weight_real, preferred_elemen...]
    another operation x4 -> x0, other arithmetic: 12.2 us -> none  [the longest x1 6.35 us: shards(): return (jnp.stack(source_list), density)]
    squeeze x3 -> x0, local copies, waits for them, and re-layouts: 8.73 us -> none  [shards(): summed = [summed_all[q_index] for q_index in range(q_count)]]
  transfers between devices with their start and end apart: 5 -> 0, of which waited for: 5 -> 0; matrix products, arithmetic and copies ran while one was open for 4% -> 0% of each run, Pallas kernels for 0% -> 0%
where the time goes in v1:
time: 161 us
  Pallas kernels  153 us (95%)
  local copies, waits for them, and re-layouts  7.49 us (5%)
    pallas_call x1, Pallas kernels, shards(): pl.pallas_call(functools.partial(kernel, sizes), out_shape=(jax.ShapeDtyp...  153 us
    unnamed x4, local copies, waits for them, and re-layouts  7.49 us

profile of v1, /device:TPU:1, one launch (start us, length us, event | category | flops | bytes accessed | tf_op | source)
XLA Modules:
  0.0 161.2 jit_solution(12999974432337812993)
XLA Ops:
  0.6 153.0 %shard_map.59 = (bf16[3,1,2,512,1024]{4,3,2,1,0:T(8,128)(2,1)}, f32[3,1024]{1,0:T(4,128)}) custom-call(s32[3,16]{1,0:T(4,128)} %partners.1, s32[16]{0:T(128)} %occupied.1, bf16[1,2,512,1024]{3,2,1,0:T(8,128)(2,1)} %orbitals.1, f32[3,2,1024]{2,1,0:T(2,128)} %potential.1), custom_call_target="tpu_custom_call" | custom-call | tf_op jit(solution)/shard_map/pallas_call | solution.py:361
  153.7 0.0 copy-start
  153.7 6.9 %copy.8 = bf16[3,1,2,512,1024]{4,3,2,1,0:T(8,128)(2,1)} copy(bf16[3,1,2,512,1024]{4,3,2,1,0:T(8,128)(2,1)} %get-tuple-element.4) | data formatting | bytes 12582912
  160.5 0.0 copy-done
  160.6 0.6 copy.9
Async XLA Ops:
  153.7 6.9 %copy-start = (f32[3,1024]{1,0:T(4,128)S(1)}, f32[3,1024]{1,0:T(4,128)}, u32[]{:S(2)}) copy-start(f32[3,1024]{1,0:T(4,128)} %get-tuple-element.5) | copy-start | bytes 36868

commit v2 on v1

--- a/solution.py
+++ b/solution.py
@@ -8,7 +8,8 @@
 from jax.sharding import PartitionSpec as P
 
 MESH = pl.DeviceIdType.MESH
-BLOCKS = 2
+BLOCKS = 4
+LAGS = (7.0, 13.0, 19.5, 26.0)
 
 
 def remote(src, dst, send_sem, recv_sem, target):
@@ -46,7 +47,6 @@
     zrecv,
     masked,
     mixer,
-    result,
     shares,
     sems,
 ):
@@ -126,12 +126,11 @@
             source, held[h].at[slot], sems["relay_s"].at[h], sems["relay_r"].at[h], beside
         ).start()
 
-    for h in range(H):
+    def start_relay(h):
         relay(h, ka, orbitals.at[0, :, rows(h, mine), :])
         held[h][ka] = orbitals[0, :, rows(h, mine), :]
-        for q in range(Q):
-            if q % H == h:
-                apply_field(q)
+
+    def pass_on(h):
         for i, (dx, dc) in enumerate(order):
             slot, _ = plane(-dx, -dc)
             remote(
@@ -169,14 +168,13 @@
         block = partner.at[q, :, pl.ds(h * M, (J - 1) * R), :]
         remote(block, block, sems["hand_s"].at[u], sems["hand_r"].at[u], beside).wait_recv()
         last = ((1,), (1,))
-        field = applied[q]
-        with_real = dot(field, partner[q, 0, h * M : (h + 1) * M, :], last)
-        with_imag = dot(field, partner[q, 1, h * M : (h + 1) * M, :], last)
-        real = volume_weight * (with_real[:B] + with_imag[B:])
-        imag = volume_weight * (with_real[B:] - with_imag[:B])
+        orbits = partner[q, :, h * M : (h + 1) * M, :].reshape(2 * M, G)
+        both = dot(applied[q], orbits, last)
+        real = volume_weight * (both[:B, :M] + both[B:, M:])
+        imag = volume_weight * (both[B:, :M] - both[:B, M:])
         for part, value in enumerate((real, imag)):
             value = value.reshape(NY, YN, M)
-            whole[:, part] = value
+            whole[u % 3, :, part] = value
             ysend[u, :, part] = value.astype(jnp.bfloat16)
         for d in range(1, NY):
             remote(
@@ -192,10 +190,10 @@
             block = yrecv.at[u]
             remote(block, block, sems["y_s"].at[u], sems["y_r"].at[u], beside).wait_recv()
         for t in range(NZ):
-            value = whole[y, :, t * ZN : (t + 1) * ZN, :]
+            value = whole[u % 3, y, :, t * ZN : (t + 1) * ZN, :]
             for d in range(NY - 1):
                 value = value + yrecv[u, d, :, t * ZN : (t + 1) * ZN, :].astype(jnp.float32)
-            quarter[t] = value
+            quarter[u % 3, t] = value
             zsend[u, t] = value.astype(jnp.bfloat16)
         for d in range(1, NZ):
             remote(
@@ -211,7 +209,7 @@
         if NZ > 1:
             block = zrecv.at[u]
             remote(block, block, sems["z_s"].at[u], sems["z_r"].at[u], beside).wait_recv()
-        value = quarter[z]
+        value = quarter[u % 3, z]
         for d in range(NZ - 1):
             value = value + zrecv[u, d].astype(jnp.float32)
         bands = h * M + lax.broadcasted_iota(jnp.int32, value.shape, 2)
@@ -251,9 +249,6 @@
         mixer[q, B : 2 * B, h * M : (h + 1) * M] = imag
         mixer[q, B : 2 * B, B + h * M : B + (h + 1) * M] = real
 
-    def out_copy(q):
-        return pltpu.make_async_copy(result.at[q], sources.at[q, 0], sems["out"].at[q])
-
     def project(q):
         own_count = occupied[ka]
         width = 256
@@ -263,8 +258,8 @@
             mixed = dot(mixer[q], partner[q, :, :, at].reshape(2 * B, width), ((1,), (0,)))
             real = applied[q, 0:B, at].astype(jnp.float32) - mixed[:B]
             imag = applied[q, B : 2 * B, at].astype(jnp.float32) - mixed[B:]
-            result[q, 0, :, at] = real.astype(jnp.bfloat16)
-            result[q, 1, :, at] = imag.astype(jnp.bfloat16)
+            sources[q, 0, 0, :, at] = real.astype(jnp.bfloat16)
+            sources[q, 0, 1, :, at] = imag.astype(jnp.bfloat16)
             term = orbitals[0, 0, :, at].astype(jnp.float32) * real
             term = term + orbitals[0, 1, :, at].astype(jnp.float32) * imag
             bands = lax.broadcasted_iota(jnp.int32, term.shape, 0)
@@ -273,7 +268,6 @@
             return 0
 
         lax.fori_loop(0, G // width, strip, 0)
-        out_copy(q).start()
         for d in range(1, K):
             remote(
                 shares.at[q, ka],
@@ -283,26 +277,32 @@
                 (lax.rem(ka + d, K), gr),
             ).start()
 
-    wait_relay(0)
-    hand_out(0)
+    def finish(u):
+        gather_y(u)
+        q, h = units[u]
+        if h == H - 1:
+            project(q)
+
+    def give(h):
+        wait_relay(h)
+        hand_out(h)
+
     count = len(units)
-    for u in range(count + 2):
-        if u < count:
-            intersect(u)
-        if 1 <= u <= count:
-            sum_z(u - 1)
-        if 2 <= u:
-            gather_y(u - 2)
-            q, h = units[u - 2]
-            if h == H - 1:
-                project(q)
-        if 1 <= u <= count:
-            gather_z(u - 1)
-        if u < count:
-            sum_y(u)
-        if u % Q == 1 and u // Q + 1 < H:
-            wait_relay(u // Q + 1)
-            hand_out(u // Q + 1)
+    start_relay(0)
+    apply_field(0)
+    beat = 22.0 / H
+    first = 30 + beat
+    steps = [(13 + beat * h, 0, pass_on, h) for h in range(H)]
+    steps += [(7 + 2 * beat * (h + 1), 1, give, h) for h in range(H)]
+    steps += [(6 + beat * h, 2, start_relay, h) for h in range(1, H)]
+    steps += [(7 + beat * q, 3, apply_field, q) for q in range(1, Q)]
+    for u in range(count):
+        arrives = first + beat * u
+        steps += [(arrives, 4, intersect, u)]
+        for i, (lag, step) in enumerate(zip(LAGS, (sum_y, sum_z, gather_z, finish))):
+            steps += [(arrives + lag, 5 + i, step, u)]
+    for _, _, step, argument in sorted(steps, key=lambda entry: entry[:2] + entry[3:]):
+        step(argument)
 
     for q in range(Q):
         block = shares.at[q, pl.ds(0, K - 1)]
@@ -313,7 +313,6 @@
         remote(block, block, sem, sem, beside).wait_send()
 
     for q in range(Q):
-        out_copy(q).wait()
         sent(shares.at[q, pl.ds(0, K - 1)], sems["share_s"].at[q])
     for h in range(H):
         sent(held[h].at[pl.ds(0, J - 1)], sems["spread_s"].at[h])
@@ -338,21 +337,20 @@
     DMA = pltpu.SemaphoreType.DMA
     sems = {name: DMA((U,)) for part in ("hand", "y", "z", "zz", "yy") for name in (part + "_s", part + "_r")}
     sems |= {"spread_s": DMA((H,)), "spread_r": DMA((H, J)), "relay_s": DMA((H,)), "relay_r": DMA((H,))}
-    sems |= {"share_s": DMA((Q,)), "share_r": DMA((Q,)), "out": DMA((Q,))}
+    sems |= {"share_s": DMA((Q,)), "share_r": DMA((Q,))}
     scratch = dict(
         held=[pltpu.VMEM((K, 2, R, G), half) for _ in range(H)],
         picked=pltpu.VMEM((U, J - 1, 2, R, G), half),
         partner=pltpu.VMEM((Q, 2, B, G), half),
         applied=pltpu.VMEM((Q, 2 * B, G), half),
-        whole=pltpu.VMEM((NY, 2, YN, M), full),
+        whole=pltpu.VMEM((3, NY, 2, YN, M), full),
         ysend=pltpu.VMEM((U, NY, 2, YN, M), half),
         yrecv=pltpu.VMEM((U, max(NY - 1, 1), 2, YN, M), half),
-        quarter=pltpu.VMEM((NZ, 2, ZN, M), full),
+        quarter=pltpu.VMEM((3, NZ, 2, ZN, M), full),
         zsend=pltpu.VMEM((U, NZ, 2, ZN, M), half),
         zrecv=pltpu.VMEM((U, max(NZ - 1, 1), 2, ZN, M), half),
         masked=pltpu.VMEM((U, NY, NZ, 2, ZN, M), half),
         mixer=pltpu.VMEM((Q, 2 * B, 2 * B), half),
-        result=pltpu.VMEM((Q, 2, B, G), half),
         shares=pltpu.VMEM((Q, K, 1, G), full),
         sems=sems,
     )
@@ -361,14 +359,14 @@
     return pl.pallas_call(
         functools.partial(kernel, sizes),
         out_shape=(
-            jax.ShapeDtypeStruct((Q, 1, 2, B, G), half),
-            jax.ShapeDtypeStruct((Q, G), full),
+            pltpu.VMEM((Q, 1, 2, B, G), half),
+            pltpu.VMEM((Q, G), full),
         ),
         in_specs=[smem, smem, vmem, vmem],
-        out_specs=(pl.BlockSpec(memory_space=pl.ANY), vmem),
+        out_specs=(vmem, vmem),
         scratch_shapes=scratch,
         compiler_params=pltpu.CompilerParams(
-            collective_id=0, has_side_effects=True, vmem_limit_bytes=64 * 1024 * 1024 - 65536
+            collective_id=0, has_side_effects=True, vmem_limit_bytes=54 * 1024 * 1024
         ),
     )(partners, occupied, orbitals, potential)
 

time: 161 us -> 145 us (0.901)
  Pallas kernels: 153 us -> 141 us
  local copies, waits for them, and re-layouts: 7.49 us -> 3.31 us
    pallas_call x1, Pallas kernels: 153 us -> 141 us  [shards(): pl.pallas_call(functools.partial(kernel, sizes), out_shape=(pltpu.VMEM((Q...]
    unnamed x4 -> x2, local copies, waits for them, and re-layouts: 7.49 us -> 3.31 us
where the time goes in v2:
time: 145 us
  Pallas kernels  141 us (97%)
  local copies, waits for them, and re-layouts  3.31 us (2%)
    pallas_call x1, Pallas kernels, shards(): pl.pallas_call(functools.partial(kernel, sizes), out_shape=(pltpu.VMEM((Q...  141 us
    unnamed x2, local copies, waits for them, and re-layouts  3.31 us

profile of v2, /device:TPU:1, one launch (start us, length us, event | category | flops | bytes accessed | tf_op | source)
XLA Modules:
  0.0 144.9 jit_solution(6423552910461026707)
XLA Ops:
  0.6 140.9 %shard_map.59 = (bf16[3,1,2,512,1024]{4,3,2,1,0:T(8,128)(2,1)S(1)}, f32[3,1024]{1,0:T(4,128)S(1)}) custom-call(s32[3,16]{1,0:T(4,128)} %partners.1, s32[16]{0:T(128)} %occupied.1, bf16[1,2,512,1024]{3,2,1,0:T(8,128)(2,1)} %orbitals.1, f32[3,2,1024]{2,1,0:T(2,128)} %potential.1), custom_call_target="tpu_custom_call" | custom-call | tf_op jit(solution)/shard_map/pallas_call | solution.py:359
  141.6 2.7 %copy.8 = bf16[3,1,2,512,1024]{4,3,2,1,0:T(8,128)(2,1)} copy(bf16[3,1,2,512,1024]{4,3,2,1,0:T(8,128)(2,1)S(1)} %get-tuple-element.2) | data formatting | bytes 12582912
  144.3 0.6 copy.9

commit v3 on v2

--- a/solution.py
+++ b/solution.py
@@ -9,7 +9,9 @@
 
 MESH = pl.DeviceIdType.MESH
 BLOCKS = 4
-LAGS = (7.0, 13.0, 19.5, 26.0)
+LAGS = (10.0, 17.0, 25.0)
+GATHERED = 35.0
+LAST = (26.0, 30.0, 34.0)
 
 
 def remote(src, dst, send_sem, recv_sem, target):
@@ -29,12 +31,16 @@
 
 def kernel(
     sizes,
+    given_partners,
+    given_occupied,
+    given_orbitals,
+    given_potential,
+    sources,
+    density,
     partners,
     occupied,
+    potential,
     orbitals,
-    potential,
-    sources,
-    density,
     held,
     picked,
     partner,
@@ -47,11 +53,12 @@
     zrecv,
     masked,
     mixer,
+    part,
     shares,
     sems,
 ):
     K, NY, NZ, Q, H = sizes
-    _, _, B, G = orbitals.shape
+    _, B, G = orbitals.shape
     NX, J = K // 4, K // 2
     M = B // H
     R = M // J
@@ -91,7 +98,21 @@
     greeted += [(ka, y * NZ + z_peer(d)) for d in range(1, NZ)]
     for target in greeted:
         pl.semaphore_signal(barrier, inc=1, device_id=target, device_id_type=MESH)
+    loads = [
+        pltpu.make_async_copy(src, dst, sems["load"].at[i])
+        for i, (src, dst) in enumerate(
+            [
+                (given_orbitals.at[0], orbitals),
+                (given_potential, potential),
+                (given_partners, partners),
+                (given_occupied, occupied),
+            ]
+        )
+    ]
+    for load in loads:
+        load.start()
     pl.semaphore_wait(barrier, len(greeted))
+    loads[0].wait()
 
     def rows(h, piece):
         return pl.ds(pl.multiple_of(h * M + piece * R, R), R)
@@ -100,7 +121,7 @@
         for i, (dx, dc) in enumerate(order):
             pk, pj = plane(dx, dc)
             remote(
-                orbitals.at[0, :, rows(h, pj), :],
+                orbitals.at[:, rows(h, pj), :],
                 held[h].at[ka],
                 sems["spread_s"].at[h],
                 sems["spread_r"].at[h, i],
@@ -113,8 +134,8 @@
         def strip(t, _):
             at = pl.ds(pl.multiple_of(t * 64, 64), 64)
             under = pl.ds(pl.multiple_of(B + t * 64, 64), 64)
-            own_real = orbitals[0, 0, at, :].astype(jnp.float32)
-            own_imag = orbitals[0, 1, at, :].astype(jnp.float32)
+            own_real = orbitals[0, at, :].astype(jnp.float32)
+            own_imag = orbitals[1, at, :].astype(jnp.float32)
             applied[q, at, :] = (real * own_real - imag * own_imag).astype(jnp.bfloat16)
             applied[q, under, :] = (real * own_imag + imag * own_real).astype(jnp.bfloat16)
             return 0
@@ -127,8 +148,8 @@
         ).start()
 
     def start_relay(h):
-        relay(h, ka, orbitals.at[0, :, rows(h, mine), :])
-        held[h][ka] = orbitals[0, :, rows(h, mine), :]
+        relay(h, ka, orbitals.at[:, rows(h, mine), :])
+        held[h][ka] = orbitals[:, rows(h, mine), :]
 
     def pass_on(h):
         for i, (dx, dc) in enumerate(order):
@@ -237,6 +258,12 @@
                 (ka, y_peer(d) * NZ + z),
             ).start()
 
+    width = 256
+
+    def columns(side, h):
+        start = side * (H - 1) * M + h * M if h < H - 1 else (2 * (H - 1) + side) * M
+        return slice(start, start + M)
+
     def gather_y(u):
         q, h = units[u]
         if NY > 1:
@@ -244,24 +271,36 @@
             remote(block, block, sems["yy_s"].at[u], sems["yy_r"].at[u], beside).wait_recv()
         real = masked[u, :, :, 0].reshape(B, M)
         imag = masked[u, :, :, 1].reshape(B, M)
-        mixer[q, 0:B, h * M : (h + 1) * M] = real
-        mixer[q, 0:B, B + h * M : B + (h + 1) * M] = -imag
-        mixer[q, B : 2 * B, h * M : (h + 1) * M] = imag
-        mixer[q, B : 2 * B, B + h * M : B + (h + 1) * M] = real
+        left, right = columns(0, h), columns(1, h)
+        mixer[q, 0:B, left] = real
+        mixer[q, 0:B, right] = -imag
+        mixer[q, B : 2 * B, left] = imag
+        mixer[q, B : 2 * B, right] = real
+
+    def prepare(q):
+        early = (H - 1) * M
+
+        def strip(t, _):
+            at = pl.ds(pl.multiple_of(t * width, width), width)
+            orbits = partner[q, :, 0:early, at].reshape(2 * early, width)
+            mixed = dot(mixer[q, :, 0 : 2 * early], orbits, ((1,), (0,)))
+            part[q, :, at] = applied[q, :, at].astype(jnp.float32) - mixed
+            return 0
+
+        lax.fori_loop(0, G // width, strip, 0)
 
     def project(q):
         own_count = occupied[ka]
-        width = 256
-
         def strip(t, _):
             at = pl.ds(pl.multiple_of(t * width, width), width)
-            mixed = dot(mixer[q], partner[q, :, :, at].reshape(2 * B, width), ((1,), (0,)))
-            real = applied[q, 0:B, at].astype(jnp.float32) - mixed[:B]
-            imag = applied[q, B : 2 * B, at].astype(jnp.float32) - mixed[B:]
+            orbits = partner[q, :, (H - 1) * M : B, at].reshape(2 * M, width)
+            mixed = dot(mixer[q, :, 2 * (H - 1) * M : 2 * B], orbits, ((1,), (0,)))
+            real = part[q, 0:B, at] - mixed[:B]
+            imag = part[q, B : 2 * B, at] - mixed[B:]
             sources[q, 0, 0, :, at] = real.astype(jnp.bfloat16)
             sources[q, 0, 1, :, at] = imag.astype(jnp.bfloat16)
-            term = orbitals[0, 0, :, at].astype(jnp.float32) * real
-            term = term + orbitals[0, 1, :, at].astype(jnp.float32) * imag
+            term = orbitals[0, :, at].astype(jnp.float32) * real
+            term = term + orbitals[1, :, at].astype(jnp.float32) * imag
             bands = lax.broadcasted_iota(jnp.int32, term.shape, 0)
             term = jnp.where(bands < own_count, term, 0.0)
             shares[q, ka, :, at] = density_weight * jnp.sum(term, axis=0, keepdims=True)
@@ -277,18 +316,14 @@
                 (lax.rem(ka + d, K), gr),
             ).start()
 
-    def finish(u):
-        gather_y(u)
-        q, h = units[u]
-        if h == H - 1:
-            project(q)
-
     def give(h):
         wait_relay(h)
         hand_out(h)
 
     count = len(units)
     start_relay(0)
+    for load in loads[1:]:
+        load.wait()
     apply_field(0)
     beat = 22.0 / H
     first = 30 + beat
@@ -299,8 +334,15 @@
     for u in range(count):
         arrives = first + beat * u
         steps += [(arrives, 4, intersect, u)]
-        for i, (lag, step) in enumerate(zip(LAGS, (sum_y, sum_z, gather_z, finish))):
+        for i, (lag, step) in enumerate(zip(LAGS, (sum_y, sum_z, gather_z))):
             steps += [(arrives + lag, 5 + i, step, u)]
+        q, h = units[u]
+        gathered = arrives + GATHERED
+        if h == H - 1:
+            gathered = first + beat * (count - 1) + LAST[q]
+        steps += [(gathered, 8, gather_y, u)]
+        if h >= H - 2:
+            steps += [(gathered + 0.01, 9, prepare if h == H - 2 else project, q)]
     for _, _, step, argument in sorted(steps, key=lambda entry: entry[:2] + entry[3:]):
         step(argument)
 
@@ -327,6 +369,18 @@
             sent(masked.at[u, 0, pl.ds(0, NZ - 1)], sems["zz_s"].at[u])
 
 
+def publish(sources, density, sources_out, density_out, sems):
+    copies = [pltpu.make_async_copy(density, density_out, sems.at[0])]
+    for i in range(2 * sources.shape[0]):
+        q, part = divmod(i, 2)
+        at = (q, 0, part)
+        copies.append(pltpu.make_async_copy(sources.at[at], sources_out.at[at], sems.at[i + 1]))
+    for copy in copies:
+        copy.start()
+    for copy in copies:
+        copy.wait()
+
+
 def shards(sizes, orbitals, potential, partners, occupied):
     K, NY, NZ, Q, H = sizes
     _, _, B, G = orbitals.shape
@@ -337,8 +391,12 @@
     DMA = pltpu.SemaphoreType.DMA
     sems = {name: DMA((U,)) for part in ("hand", "y", "z", "zz", "yy") for name in (part + "_s", part + "_r")}
     sems |= {"spread_s": DMA((H,)), "spread_r": DMA((H, J)), "relay_s": DMA((H,)), "relay_r": DMA((H,))}
-    sems |= {"share_s": DMA((Q,)), "share_r": DMA((Q,))}
+    sems |= {"share_s": DMA((Q,)), "share_r": DMA((Q,)), "load": DMA((4,))}
     scratch = dict(
+        partners=pltpu.SMEM((Q, K), jnp.int32),
+        occupied=pltpu.SMEM((K,), jnp.int32),
+        potential=pltpu.VMEM((Q, 2, G), full),
+        orbitals=pltpu.VMEM((2, B, G), half),
         held=[pltpu.VMEM((K, 2, R, G), half) for _ in range(H)],
         picked=pltpu.VMEM((U, J - 1, 2, R, G), half),
         partner=pltpu.VMEM((Q, 2, B, G), half),
@@ -351,24 +409,36 @@
         zrecv=pltpu.VMEM((U, max(NZ - 1, 1), 2, ZN, M), half),
         masked=pltpu.VMEM((U, NY, NZ, 2, ZN, M), half),
         mixer=pltpu.VMEM((Q, 2 * B, 2 * B), half),
+        part=pltpu.VMEM((Q, 2 * B, G), full),
         shares=pltpu.VMEM((Q, K, 1, G), full),
         sems=sems,
     )
     vmem = pl.BlockSpec(memory_space=pltpu.VMEM)
-    smem = pl.BlockSpec(memory_space=pltpu.SMEM)
-    return pl.pallas_call(
+    sources, density = pl.pallas_call(
         functools.partial(kernel, sizes),
         out_shape=(
             pltpu.VMEM((Q, 1, 2, B, G), half),
             pltpu.VMEM((Q, G), full),
         ),
-        in_specs=[smem, smem, vmem, vmem],
+        in_specs=[pl.BlockSpec(memory_space=pl.ANY)] * 4,
         out_specs=(vmem, vmem),
         scratch_shapes=scratch,
         compiler_params=pltpu.CompilerParams(
-            collective_id=0, has_side_effects=True, vmem_limit_bytes=54 * 1024 * 1024
+            collective_id=0, has_side_effects=True, vmem_limit_bytes=57 * 1024 * 1024
         ),
     )(partners, occupied, orbitals, potential)
+    anywhere = pl.BlockSpec(memory_space=pl.ANY)
+    return pl.pallas_call(
+        publish,
+        out_shape=(
+            jax.ShapeDtypeStruct((Q, 1, 2, B, G), half),
+            jax.ShapeDtypeStruct((Q, G), full),
+        ),
+        in_specs=[anywhere] * 2,
+        out_specs=(anywhere, anywhere),
+        scratch_shapes=[DMA((2 * Q + 1,))],
+        compiler_params=pltpu.CompilerParams(vmem_limit_bytes=1024 * 1024),
+    )(sources, density)
 
 
 def solution(mesh, ways=None):

time: 145 us -> 137 us (0.945)
  Pallas kernels: 141 us -> 136 us
  local copies, waits for them, and re-layouts: 3.31 us -> 0 us
    pallas_call x1, Pallas kernels: 141 us -> 133 us  [shards(): pl.pallas_call(functools.partial(kernel, sizes), out_shape=(pltpu.VMEM((Q...]
    unnamed x2 -> x0, local copies, waits for them, and re-layouts: 3.31 us -> none
    pallas_call x0 -> x1, Pallas kernels: none -> 2.73 us  [shards(): pl.pallas_call(publish, out_shape=(jax.ShapeDtypeStruct((Q, 1, 2, B, G),...]
where the time goes in v3:
time: 137 us
  Pallas kernels  136 us (99%)
    pallas_call x1, Pallas kernels, shards(): pl.pallas_call(functools.partial(kernel, sizes), out_shape=(pltpu.VMEM((Q...  133 us

profile of v3, /device:TPU:1, one launch (start us, length us, event | category | flops | bytes accessed | tf_op | source)
XLA Modules:
  0.0 136.8 jit_solution(16920337264965040342)
XLA Ops:
  0.6 133.2 %shard_map.59 = (bf16[3,1,2,512,1024]{4,3,2,1,0:T(8,128)(2,1)S(1)}, f32[3,1024]{1,0:T(4,128)S(1)}) custom-call(s32[3,16]{1,0:T(4,128)} %given_partners.1, s32[16]{0:T(128)} %given_occupied.1, bf16[1,2,512,1024]{3,2,1,0:T(8,128)(2,1)} %given_orbitals.1, f32[3,2,1024]{2,1,0:T(2,128)} %given_potential.1), custom_call_target="tpu_custom_call" | custom-call | tf_op jit(solution)/shard_map/pallas_call | solution.py:417
  133.9 2.7 %shard_map.60 = (bf16[3,1,2,512,1024]{4,3,2,1,0:T(8,128)(2,1)}, f32[3,1024]{1,0:T(4,128)}) custom-call(bf16[3,1,2,512,1024]{4,3,2,1,0:T(8,128)(2,1)S(1)} %get-tuple-element.4.sources, f32[3,1024]{1,0:T(4,128)S(1)} %get-tuple-element.5.density), custom_call_target="tpu_custom_call" | custom-call | tf_op jit(solution)/shard_map/pallas_call | solution.py:431

commit v4 on v3

--- a/solution.py
+++ b/solution.py
@@ -346,16 +346,9 @@
     for _, _, step, argument in sorted(steps, key=lambda entry: entry[:2] + entry[3:]):
         step(argument)
 
-    for q in range(Q):
-        block = shares.at[q, pl.ds(0, K - 1)]
-        remote(block, block, sems["share_s"].at[q], sems["share_r"].at[q], beside).wait_recv()
-        density[q : q + 1, :] = jnp.sum(shares[q], axis=0)
-
     def sent(block, sem):
         remote(block, block, sem, sem, beside).wait_send()
 
-    for q in range(Q):
-        sent(shares.at[q, pl.ds(0, K - 1)], sems["share_s"].at[q])
     for h in range(H):
         sent(held[h].at[pl.ds(0, J - 1)], sems["spread_s"].at[h])
         sent(held[h].at[pl.ds(0, J)], sems["relay_s"].at[h])
@@ -367,6 +360,13 @@
         if NZ > 1:
             sent(zrecv.at[u], sems["z_s"].at[u])
             sent(masked.at[u, 0, pl.ds(0, NZ - 1)], sems["zz_s"].at[u])
+
+    for q in range(Q):
+        block = shares.at[q, pl.ds(0, K - 1)]
+        remote(block, block, sems["share_s"].at[q], sems["share_r"].at[q], beside).wait_recv()
+        density[q : q + 1, :] = jnp.sum(shares[q], axis=0)
+    for q in range(Q):
+        sent(shares.at[q, pl.ds(0, K - 1)], sems["share_s"].at[q])
 
 
 def publish(sources, density, sources_out, density_out, sems):

time: 137 us -> 137 us (level)
  no operation moved by 1% of the time
where the time goes in v4:
time: 137 us
  Pallas kernels  136 us (99%)
    pallas_call x1, Pallas kernels, shards(): pl.pallas_call(functools.partial(kernel, sizes), out_shape=(pltpu.VMEM((Q...  133 us

profile of v4, /device:TPU:1, one launch (start us, length us, event | category | flops | bytes accessed | tf_op | source)
XLA Modules:
  0.0 136.7 jit_solution(13642264559088941412)
XLA Ops:
  0.6 133.1 %shard_map.59 = (bf16[3,1,2,512,1024]{4,3,2,1,0:T(8,128)(2,1)S(1)}, f32[3,1024]{1,0:T(4,128)S(1)}) custom-call(s32[3,16]{1,0:T(4,128)} %given_partners.1, s32[16]{0:T(128)} %given_occupied.1, bf16[1,2,512,1024]{3,2,1,0:T(8,128)(2,1)} %given_orbitals.1, f32[3,2,1024]{2,1,0:T(2,128)} %given_potential.1), custom_call_target="tpu_custom_call" | custom-call | tf_op jit(solution)/shard_map/pallas_call | solution.py:417
  133.8 2.7 %shard_map.60 = (bf16[3,1,2,512,1024]{4,3,2,1,0:T(8,128)(2,1)}, f32[3,1024]{1,0:T(4,128)}) custom-call(bf16[3,1,2,512,1024]{4,3,2,1,0:T(8,128)(2,1)S(1)} %get-tuple-element.4.sources, f32[3,1024]{1,0:T(4,128)S(1)} %get-tuple-element.5.density), custom_call_target="tpu_custom_call" | custom-call | tf_op jit(solution)/shard_map/pallas_call | solution.py:431
